TPU v7x, 32 devices: a whole 2x2x4 slice. The times are simulated.
32 devices in a mesh: batch: 8 (over z, y), mp: 4 (over x, core).
Axes of the slice: x: 2, y: 2, z: 4, core: 2. Of those that a mesh axis runs over, the one named last changes fastest.
Arguments:
- lookup_ids: int32 [64, 16384], P('batch'), may hold values from 0 to 8191
- table_feature: int32 [64], replicated, may hold values from 0 to 63, each once
- tables: bfloat16 [64, 8192, 128], P('batch'), may hold values from -6 to 6
- cross_down: bfloat16 [2, 8192, 512], P(None, 'mp'), may hold values from -0.0625 to 0.0625
- cross_up: bfloat16 [2, 512, 8192], P(None, None, 'mp'), may hold values from -0.25 to 0.25
- cross_bias: float32 [2, 8192], P(None, 'mp'), may hold values from -3 to 3
Outputs:
- crossed: bfloat16 [16384, 8192], P('batch', 'mp')
Inputs may be any that keep to these rules, and one draw needn't show every extreme that they name: `table_feature`: each number appears once.
All inputs are finite; a program needn't handle non-finite values.
Results may differ from a plain program's by a relative error of at most 0.015.
Values may be sent and summed in bfloat16 or wider, within the bound.
A program may use at most 128 MiB of HBM per device.

v0:
```python
import jax
import jax.numpy as jnp
from jax import lax
from jax.sharding import PartitionSpec as P


def per_device(lookup_ids, table_feature, tables, cross_down, cross_up, cross_bias):
    slots_local = tables.shape[0]
    feats = table_feature.shape[0]
    sources = lax.axis_size("batch")
    groups = lax.axis_size("mp")
    examples_local = lookup_ids.shape[1] // sources
    share = examples_local // groups
    start = lax.axis_index("mp") * share
    by_owner = lookup_ids.reshape(slots_local, sources, examples_local)
    wanted = lax.dynamic_slice_in_dim(by_owner, start, share, 2)
    looked = jnp.stack(
        [
            jnp.take(tables[slot], wanted[slot].reshape(sources * share), axis=0)
            for slot in range(slots_local)
        ],
        axis=1,
    )
    looked = looked.reshape(sources, share, slots_local, tables.shape[2])
    received = lax.all_to_all(
        lax.all_to_all(looked, "batch", split_axis=0, concat_axis=0, tiled=True),
        "mp",
        split_axis=3,
        concat_axis=1,
        tiled=True,
    )
    emb_local = received.shape[3]
    unfolded = jnp.transpose(received, (1, 0, 2, 3)).reshape(examples_local, feats, emb_local)
    placing = (table_feature[:, None] == jnp.arange(feats, dtype=jnp.int32)[None, :]).astype(
        jnp.bfloat16
    )
    ordered = jnp.einsum("rse,sf->ref", unfolded, placing, preferred_element_type=jnp.float32)
    embedded = ordered.astype(jnp.bfloat16).reshape(examples_local, emb_local * feats)
    embedded_wide = embedded.astype(jnp.float32)
    state = embedded
    for layer in range(len(cross_down)):
        weight_down = cross_down[layer]
        term = jnp.dot(state, weight_down, preferred_element_type=jnp.float32)
        term = term.astype(jnp.bfloat16).astype(jnp.float32)
        low = lax.psum(term.astype(jnp.bfloat16), "mp")
        high = (
            jnp.dot(low, cross_up[layer], preferred_element_type=jnp.float32)
            + cross_bias[layer][None, :]
        )
        state = (embedded_wide * high + state.astype(jnp.float32)).astype(jnp.bfloat16)
    return state


def solution(mesh):
    return jax.shard_map(
        per_device,
        mesh=mesh,
        in_specs=(
            P("batch", None),
            P(),
            P("batch", None, None),
            P(None, "mp", None),
            P(None, None, "mp"),
            P(None, "mp"),
        ),
        out_specs=P("batch", "mp"),
        check_vma=False,
    )
```

profile of v0, /device:TPU:0, one launch (start us, length us, event | category | flops | bytes accessed | tf_op | source)
XLA Modules:
  0.0 718.1 jit_solution(7940920189103681202)
XLA Ops:
  6.5 2.1 constant_dynamic-slice_fusion.7
  8.9 11.4 %slice_bitcast_fusion = (bf16[8192,128]{1,0:T(8,128)(2,1)}, bf16[8192,128]{1,0:T(8,128)(2,1)}, bf16[8192,128]{1,0:T(8,128)(2,1)}, bf16[8192,128]{1,0:T(8,128)(2,...) fusion(bf16[8,8192,128]{2,1,0:T(8,128)(2,1)} %param.10), kind=kLoop, calls=%fused_computation.27 | loop fusion | bytes 33554432 | tf_op jit(solution)/shard_map/squeeze | solution.py:19
  20.4 12.9 %gather_fusion.1 = bf16[4096,128]{1,0:T(8,128)(2,1)S(1)} fusion(bf16[8192,128]{1,0:T(8,128)(2,1)} %get-tuple-element.11, s32[4096]{0:T(1024)S(1)} %fusion.21), kind=kCustom, calls=%fused_computation.1.clone | custom fusion | bytes 2113536 | tf_op jit(solution)/shard_map/jit(_take)/gather | solution.py:19
  33.3 2.9 broadcast_select_fusion.6
  36.2 6.0 copy.42
  42.1 12.9 %gather_fusion.2 = bf16[4096,128]{1,0:T(8,128)(2,1)S(1)} fusion(bf16[8192,128]{1,0:T(8,128)(2,1)} %get-tuple-element.10, s32[4096]{0:T(1024)S(1)} %fusion.22), kind=kCustom, calls=%fused_computation.2.clone | custom fusion | bytes 2113536 | tf_op jit(solution)/shard_map/jit(_take)/gather | solution.py:19
  55.0 2.9 broadcast_select_fusion.5
  57.9 5.9 copy.43
  63.9 12.9 %gather_fusion.3 = bf16[4096,128]{1,0:T(8,128)(2,1)S(1)} fusion(bf16[8192,128]{1,0:T(8,128)(2,1)} %get-tuple-element.9, s32[4096]{0:T(1024)S(1)} %fusion.23), kind=kCustom, calls=%fused_computation.3.clone | custom fusion | bytes 2113536 | tf_op jit(solution)/shard_map/jit(_take)/gather | solution.py:19
  76.8 2.9 broadcast_select_fusion.4
  79.7 6.0 copy.44
  85.7 12.9 %gather_fusion.4 = bf16[4096,128]{1,0:T(8,128)(2,1)S(1)} fusion(bf16[8192,128]{1,0:T(8,128)(2,1)} %get-tuple-element.8, s32[4096]{0:T(1024)S(1)} %fusion.24), kind=kCustom, calls=%fused_computation.4.clone | custom fusion | bytes 2113536 | tf_op jit(solution)/shard_map/jit(_take)/gather | solution.py:19
  98.6 2.9 broadcast_select_fusion.3
  101.5 6.0 copy.45
  107.5 12.9 %gather_fusion.5 = bf16[4096,128]{1,0:T(8,128)(2,1)S(1)} fusion(bf16[8192,128]{1,0:T(8,128)(2,1)} %get-tuple-element.7, s32[4096]{0:T(1024)S(1)} %fusion.25), kind=kCustom, calls=%fused_computation.5.clone | custom fusion | bytes 2113536 | tf_op jit(solution)/shard_map/jit(_take)/gather | solution.py:19
  120.4 2.9 broadcast_select_fusion.2
  123.3 6.0 copy.46
  129.3 12.9 %gather_fusion.6 = bf16[4096,128]{1,0:T(8,128)(2,1)S(1)} fusion(bf16[8192,128]{1,0:T(8,128)(2,1)} %get-tuple-element.13, s32[4096]{0:T(1024)S(1)} %fusion.26), kind=kCustom, calls=%fused_computation.6.clone | custom fusion | bytes 2113536 | tf_op jit(solution)/shard_map/jit(_take)/gather | solution.py:19
  142.2 2.9 broadcast_select_fusion.1
  145.1 5.9 copy.47
  151.0 12.9 %gather_fusion.7 = bf16[4096,128]{1,0:T(8,128)(2,1)S(1)} fusion(bf16[8192,128]{1,0:T(8,128)(2,1)} %get-tuple-element.6, s32[4096]{0:T(1024)S(1)} %fusion.27), kind=kCustom, calls=%fused_computation.7.clone | custom fusion | bytes 2113536 | tf_op jit(solution)/shard_map/jit(_take)/gather | solution.py:19
  163.9 2.9 broadcast_select_fusion
  166.8 6.0 copy.48
  172.8 12.1 %gather_fusion = bf16[4096,128]{1,0:T(8,128)(2,1)S(1)} fusion(bf16[8192,128]{1,0:T(8,128)(2,1)S(1)} %get-tuple-element.12, s32[4096]{0:T(1024)S(1)} %fusion.20), kind=kCustom, calls=%fused_computation.clone | custom fusion | bytes 2113536 | tf_op jit(solution)/shard_map/jit(_take)/gather | solution.py:19
  184.9 2.9 broadcast_select_fusion.7
  187.8 5.9 copy.41
  193.8 42.8 %stack.35 = bf16[8,512,8,128]{1,2,3,0:T(8,128)(2,1)} concatenate(bf16[8,512,1,128]{1,2,3,0:T(2,128)(2,1)} %copy.41, bf16[8,512,1,128]{1,2,3,0:T(2,128)(2,1)S(1)} %copy-done.1, bf16[8,512,1,128]{1,2,3,0:T(2,128)(2,1)} %copy.43, bf16[8,512,1,128]{1,2,3,0:T(2,128)(2,1)} %copy.44, bf16[8,512,1,128]{1,2,3,0:T(2,128)(2,1)} %copy.45, bf16[8,512,1,128]{1,2,3,0:T(2,128)(2,1)} %copy.46, ...), dimensions={2} | concatenate | bytes 16777216 | tf_op jit(solution)/shard_map/stack | solution.py:17
  236.5 190.6 %all_to_all.23 = bf16[8,512,8,128]{1,2,3,0:T(8,128)(2,1)} all-to-all(bf16[8,512,8,128]{1,2,3,0:T(8,128)(2,1)} %stack.35), channel_id=1, replica_groups=mesh['batch'=8,'mp'=4] {'batch'}, dimensions={0} | all-to-all | bytes 16777216 | tf_op jit(solution)/shard_map/all_to_all | solution.py:26
  427.2 8.1 %copy.49 = bf16[8,512,8,128]{1,2,0,3:T(8,128)(2,1)} copy(bf16[8,512,8,128]{1,2,3,0:T(8,128)(2,1)} %all_to_all.23) | data formatting | bytes 16777216 | tf_op jit(solution)/shard_map/all_to_all | solution.py:26
  435.2 97.2 %all_to_all.24 = bf16[8,512,8,128]{1,2,0,3:T(8,128)(2,1)S(1)} all-to-all(bf16[8,512,8,128]{1,2,0,3:T(8,128)(2,1)} %copy.49), channel_id=1, replica_groups=mesh['batch'=8,'mp'=4] {'mp'}, dimensions={3} | all-to-all | bytes 16777216 | tf_op jit(solution)/shard_map/all_to_all | solution.py:25
  532.4 7.3 %copy.51 = bf16[8,4,512,8,32]{2,1,4,3,0:T(4,128)(2,1)} copy(bf16[8,4,512,8,32]{2,3,0,4,1:T(8,128)(2,1)S(1)} %bitcast.69) | data formatting | bytes 16777216 | tf_op jit(solution)/shard_map/all_to_all | solution.py:25
  539.7 14.4 %all_to_all.20 = bf16[8,2048,8,32]{1,3,2,0:T(8,128)(2,1)} reshape(bf16[8,4,512,8,32]{2,1,4,3,0:T(4,128)(2,1)} %copy.51) | data formatting | bytes 16777216 | tf_op jit(solution)/shard_map/all_to_all | solution.py:25
  554.1 10.1 %fusion.6 = bf16[2048,32,64]{0,2,1:T(8,128)(2,1)S(1)} fusion(bf16[2048,8,8,32]{0,3,2,1:T(8,128)(2,1)} %bitcast.68, s32[64]{0:T(128)S(1)} %copy-done.3), kind=kOutput, calls=%fused_computation.16 | convolution fusion | flops 541069312 | bytes 16777472 | tf_op jit(solution)/shard_map/rse,sf->ref/dot_general | solution.py:37
  564.2 0.0 copy-start
  564.2 3.4 copy-done
  567.6 7.3 %convolution_convert_fusion.1 = bf16[2048,512]{1,0:T(8,128)(2,1)} fusion(bf16[2048,2048]{0,1:T(8,128)(2,1)S(1)} %bitcast.66, bf16[2,2048,512]{2,1,0:T(8,128)(2,1)} %param.11), kind=kOutput, calls=%fused_computation.18 | convolution fusion | flops 4296015872 | bytes 12582912 | tf_op jit(solution)/shard_map/dot_general | solution.py:43
  574.9 0.0 all-reduce.3.cloned.1.call-update
  575.0 0.0 all-reduce.5.cloned.1.call-start
  575.0 11.9 %copy.53 = bf16[2048,2048]{1,0:T(8,128)(2,1)} copy(bf16[2048,2048]{0,1:T(8,128)(2,1)} %bitcast.67) | data formatting | bytes 16777216 | tf_op jit(solution)/shard_map/reshape | solution.py:38
  586.9 37.5 %all-reduce.3.cloned.1.call-done = bf16[2048,512]{1,0:T(8,128)(2,1)} async-done(((bf16[2048,512]{1,0:T(8,128)(2,1)}), bf16[2048,512]{1,0:T(8,128)(2,1)}) %all-reduce.3.cloned.1.call-update) | async-done | bytes 2097168 | tf_op jit(solution)/shard_map/psum | solution.py:45
  624.4 9.9 %fusion.2 = bf16[2048,2048]{1,0:T(8,128)(2,1)S(1)} fusion(bf16[2048,2048]{1,0:T(8,128)(2,1)} %copy.53, f32[2048]{0:T(1024)S(1)} %bitcast.96, bf16[2048,512]{1,0:T(8,128)(2,1)} %all-reduce.3.cloned.1.call-done, bf16[2,512,2048]{2,1,0:T(8,128)(2,1)} %param.12), kind=kOutput, calls=%fused_computation.12 | convolution fusion | flops 4315938816 | bytes 20979712 | tf_op jit(solution)/shard_map/dot_general | solution.py:47
  634.4 0.0 copy-start.5
  634.4 3.4 copy-done.5
  637.8 0.0 copy-done.4
  637.8 5.9 convolution_convert_fusion
  643.7 0.0 all-reduce.5.cloned.1.call-update
  643.8 51.6 %all-reduce.5.cloned.1.call-done = bf16[2048,512]{1,0:T(8,128)(2,1)} async-done(((bf16[2048,512]{1,0:T(8,128)(2,1)}), bf16[2048,512]{1,0:T(8,128)(2,1)}) %all-reduce.5.cloned.1.call-update) | async-done | bytes 2097168 | tf_op jit(solution)/shard_map/psum | solution.py:45
  695.4 15.9 %fusion.1 = bf16[2048,2048]{1,0:T(8,128)(2,1)} fusion(bf16[2048,2048]{1,0:T(8,128)(2,1)} %copy.53, bf16[2048,2048]{1,0:T(8,128)(2,1)} %copy-done.5, f32[2048]{0:T(1024)S(1)} %bitcast.95, bf16[2048,512]{1,0:T(8,128)(2,1)} %all-reduce.5.cloned.1.call-done, bf16[2,512,2048]{2,1,0:T(8,128)(2,1)} %param.12), kind=kOutput, calls=%fused_computation.11 | convolution fusion | flops 4320133120 | bytes 29368320 | tf_op jit(solution)/shard_map/dot_general | solution.py:47
  (25 shorter events, 0.2 us)
Async XLA Ops:
  6.5 617.9 %all-reduce.3.cloned.1.call-start = ((), (), s32[]{:S(2)}) async-start(), calls=%async_computation.2 | async-start | bytes 4194304 | tf_op jit(solution)/shard_map/psum | solution.py:45
  184.9 8.8 %copy-start.1 = (bf16[8,512,1,128]{1,2,3,0:T(2,128)(2,1)S(1)}, bf16[8,512,1,128]{1,2,3,0:T(2,128)(2,1)}, u32[]{:S(2)}) copy-start(bf16[8,512,1,128]{1,2,3,0:T(2,128)(2,1)} %copy.42) | copy-start | bytes 3145732
  539.7 14.4 %copy-start.3 = (s32[64]{0:T(128)S(1)}, s32[64]{0:T(128)}, u32[]{:S(2)}) copy-start(s32[64]{0:T(128)} %param.9) | copy-start | bytes 772
  564.2 3.4 copy-start
  567.6 7.4 %copy-start.2 = (f32[2,2048]{1,0:T(2,128)S(1)}, f32[2,2048]{1,0:T(2,128)}, u32[]{:S(2)}) copy-start(f32[2,2048]{1,0:T(2,128)} %param.13) | copy-start | bytes 49156
  575.0 120.4 %all-reduce.5.cloned.1.call-start = ((), (), s32[]{:S(2)}) async-start(), calls=%async_computation.3 | async-start | bytes 4194304 | tf_op jit(solution)/shard_map/psum | solution.py:45
  624.4 13.3 %copy-start.4 = (bf16[2,2048,512]{2,1,0:T(8,128)(2,1)S(1)}, bf16[2,2048,512]{2,1,0:T(8,128)(2,1)}, u32[]{:S(2)}) copy-start(bf16[2,2048,512]{2,1,0:T(8,128)(2,1)} %param.11) | copy-start | bytes 12582916
  634.4 3.4 copy-start.5
Sparse Core Ops, SparseCore 0:
  575.1 49.3 all-reduce.2
  643.9 51.4 all-reduce.4
where the time goes:
time: 725 us; the launch traced here: 718 us
  blocking collectives  288 us (40%)
  local copies, waits for them, and re-layouts  255 us (35%)
  waiting for transfers between devices  89.2 us (12%)
  matrix products  49.2 us (7%)
  other arithmetic  23.4 us (3%)
  between operations  13.7 us (2%)
    all_to_all x1, blocking collectives, per_device(): lax.all_to_all(looked, 'batch', split_axis=0, concat_axis=0, tiled=True)  191 us
    gather x8, local copies, waits for them, and re-layouts, per_device(): jnp.take(tables[slot], wanted[slot].reshape(sources * share), axis=0)  102 us
    all_to_all x1, blocking collectives, per_device(): lax.all_to_all(lax.all_to_all(looked, 'batch', split_axis=0, concat_axis=...  97.2 us
    another operation x9, local copies, waits for them, and re-layouts, per_device(): jnp.stack([jnp.take(tables[slot], wanted[slot].reshape(sources * share),...  90.5 us
    psum x2, waiting for transfers between devices, per_device(): low = lax.psum(term.astype(jnp.bfloat16), 'mp')  89.1 us
    dot_general x2, matrix products, per_device(): jnp.dot(low, cross_up[layer], preferred_element_type=jnp.float32)  25.8 us
    select_n x8, other arithmetic, per_device(): jnp.take(tables[slot], wanted[slot].reshape(sources * share), axis=0)  23.3 us
    all_to_all x2, local copies, waits for them, and re-layouts, per_device(): lax.all_to_all(lax.all_to_all(looked, 'batch', split_axis=0, concat_axis=...  21.7 us
  transfers between devices with their start and end apart: 2, of which 2 were waited for; matrix products, arithmetic and copies ran while one was open for 2% of the time, Pallas kernels for 0%

commit v1 on v0

--- a/solution.py
+++ b/solution.py
@@ -22,12 +22,20 @@
         axis=1,
     )
     looked = looked.reshape(sources, share, slots_local, tables.shape[2])
-    received = lax.all_to_all(
-        lax.all_to_all(looked, "batch", split_axis=0, concat_axis=0, tiled=True),
-        "mp",
-        split_axis=3,
-        concat_axis=1,
-        tiled=True,
+    received = jnp.concatenate(
+        lax.all_to_all(
+            jnp.stack(
+                jnp.split(
+                    lax.all_to_all(looked, "batch", split_axis=0, concat_axis=0, tiled=True),
+                    lax.axis_size("mp"),
+                    axis=3,
+                )
+            ),
+            "mp",
+            0,
+            0,
+        ),
+        axis=1,
     )
     emb_local = received.shape[3]
     unfolded = jnp.transpose(received, (1, 0, 2, 3)).reshape(examples_local, feats, emb_local)

time: 725 us -> 667 us (0.920)
  local copies, waits for them, and re-layouts: 255 us -> 196 us
    another operation x9 -> x1, local copies, waits for them, and re-layouts: 90.5 us -> 1.15 us  [per_device(): jnp.stack([jnp.take(tables[slot], wanted[slot].reshape(sources * share),...]
    another operation x0 -> x5, local copies, waits for them, and re-layouts: none -> 43.8 us  [per_device(): jnp.stack(jnp.split(lax.all_to_all(looked, 'batch', split_axis=0, concat_...]
    all_to_all x3 -> x0, local copies, waits for them, and re-layouts: 29.7 us -> none  [the longest x2 21.7 us: per_device(): lax.all_to_all(lax.all_to_all(looked, 'batch', split_axis=0, concat_axis=...]
    reshape x0 -> x1, local copies, waits for them, and re-layouts: none -> 8.12 us  [per_device(): jnp.concatenate(lax.all_to_all(jnp.stack(jnp.split(lax.all_to_all(looked,...]
    unnamed x12 -> x17, local copies, waits for them, and re-layouts: 6.8 us -> 14.9 us
where the time goes in v1:
time: 667 us; the launch traced here: 657 us
  blocking collectives  288 us (43%)
  local copies, waits for them, and re-layouts  196 us (29%)
  waiting for transfers between devices  89.4 us (13%)
  matrix products  49.4 us (7%)
  other arithmetic  21.1 us (3%)
  between operations  13.9 us (2%)
    all_to_all x1, blocking collectives, per_device(): lax.all_to_all(looked, 'batch', split_axis=0, concat_axis=0, tiled=True)  191 us
    gather x8, local copies, waits for them, and re-layouts, per_device(): jnp.take(tables[slot], wanted[slot].reshape(sources * share), axis=0)  102 us
    all_to_all x1, blocking collectives, per_device(): lax.all_to_all(jnp.stack(jnp.split(lax.all_to_all(looked, 'batch', split_...  96.8 us
    psum x2, waiting for transfers between devices, per_device(): low = lax.psum(term.astype(jnp.bfloat16), 'mp')  89.3 us
    another operation x5, local copies, waits for them, and re-layouts, per_device(): jnp.stack(jnp.split(lax.all_to_all(looked, 'batch', split_axis=0, concat_...  43.8 us
    dot_general x2, matrix products, per_device(): jnp.dot(low, cross_up[layer], preferred_element_type=jnp.float32)  25.8 us
    select_n x8, other arithmetic, per_device(): jnp.take(tables[slot], wanted[slot].reshape(sources * share), axis=0)  17.2 us
    unnamed x17, local copies, waits for them, and re-layouts  14.9 us
  transfers between devices with their start and end apart: 2, of which 2 were waited for; matrix products, arithmetic and copies ran while one was open for 2% of the time, Pallas kernels for 0%

profile of v1, /device:TPU:0, one launch (start us, length us, event | category | flops | bytes accessed | tf_op | source)
XLA Modules:
  0.0 657.3 jit_solution(1250544411446974405)
XLA Ops:
  6.5 2.1 constant_dynamic-slice_fusion.7
  8.9 11.5 %slice_bitcast_fusion.4 = (bf16[8192,128]{1,0:T(8,128)(2,1)S(1)}, bf16[8192,128]{1,0:T(8,128)(2,1)}, bf16[8192,128]{1,0:T(8,128)(2,1)}, bf16[8192,128]{1,0:T(8,1...) fusion(bf16[8,8192,128]{2,1,0:T(8,128)(2,1)} %param.10), kind=kLoop, calls=%fused_computation.32 | loop fusion | bytes 33554432 | tf_op jit(solution)/shard_map/squeeze | solution.py:19
  20.3 12.9 %gather_fusion = bf16[4096,128]{1,0:T(8,128)(2,1)S(1)} fusion(bf16[8192,128]{1,0:T(8,128)(2,1)} %get-tuple-element.12, s32[4096]{0:T(1024)S(1)} %get-tuple-element.28), kind=kCustom, calls=%fused_computation.clone | custom fusion | bytes 2113536 | tf_op jit(solution)/shard_map/jit(_take)/gather | solution.py:19
  33.2 2.1 broadcast_select_fusion.7
  35.4 1.2 constant_dynamic-update-slice_fusion.7
  36.5 12.9 %gather_fusion.1 = bf16[4096,128]{1,0:T(8,128)(2,1)S(1)} fusion(bf16[8192,128]{1,0:T(8,128)(2,1)} %get-tuple-element.11, s32[4096]{0:T(1024)S(1)} %get-tuple-element.29), kind=kCustom, calls=%fused_computation.1.clone | custom fusion | bytes 2113536 | tf_op jit(solution)/shard_map/jit(_take)/gather | solution.py:19
  49.4 2.1 broadcast_select_fusion.6
  51.6 1.2 constant_dynamic-update-slice_fusion.6
  52.7 12.9 %gather_fusion.2 = bf16[4096,128]{1,0:T(8,128)(2,1)S(1)} fusion(bf16[8192,128]{1,0:T(8,128)(2,1)} %get-tuple-element.10, s32[4096]{0:T(1024)S(1)} %get-tuple-element.30), kind=kCustom, calls=%fused_computation.2.clone | custom fusion | bytes 2113536 | tf_op jit(solution)/shard_map/jit(_take)/gather | solution.py:19
  65.6 2.1 broadcast_select_fusion.5
  67.8 1.2 constant_dynamic-update-slice_fusion.5
  69.0 12.9 %gather_fusion.3 = bf16[4096,128]{1,0:T(8,128)(2,1)S(1)} fusion(bf16[8192,128]{1,0:T(8,128)(2,1)} %get-tuple-element.9, s32[4096]{0:T(1024)S(1)} %get-tuple-element.31), kind=kCustom, calls=%fused_computation.3.clone | custom fusion | bytes 2113536 | tf_op jit(solution)/shard_map/jit(_take)/gather | solution.py:19
  81.9 2.1 broadcast_select_fusion.4
  84.0 1.2 constant_dynamic-update-slice_fusion.4
  85.2 12.9 %gather_fusion.4 = bf16[4096,128]{1,0:T(8,128)(2,1)S(1)} fusion(bf16[8192,128]{1,0:T(8,128)(2,1)} %get-tuple-element.8, s32[4096]{0:T(1024)S(1)} %get-tuple-element.32), kind=kCustom, calls=%fused_computation.4.clone | custom fusion | bytes 2113536 | tf_op jit(solution)/shard_map/jit(_take)/gather | solution.py:19
  98.1 2.1 broadcast_select_fusion.3
  100.2 1.2 constant_dynamic-update-slice_fusion.3
  101.4 12.9 %gather_fusion.5 = bf16[4096,128]{1,0:T(8,128)(2,1)S(1)} fusion(bf16[8192,128]{1,0:T(8,128)(2,1)} %get-tuple-element.7, s32[4096]{0:T(1024)S(1)} %get-tuple-element.33), kind=kCustom, calls=%fused_computation.5.clone | custom fusion | bytes 2113536 | tf_op jit(solution)/shard_map/jit(_take)/gather | solution.py:19
  114.3 2.1 broadcast_select_fusion.2
  116.4 1.2 constant_dynamic-update-slice_fusion.2
  117.6 12.9 %gather_fusion.6 = bf16[4096,128]{1,0:T(8,128)(2,1)S(1)} fusion(bf16[8192,128]{1,0:T(8,128)(2,1)} %get-tuple-element.13, s32[4096]{0:T(1024)S(1)} %get-tuple-element.34), kind=kCustom, calls=%fused_computation.6.clone | custom fusion | bytes 2113536 | tf_op jit(solution)/shard_map/jit(_take)/gather | solution.py:19
  130.5 2.1 broadcast_select_fusion.1
  132.6 1.2 constant_dynamic-update-slice_fusion.1
  133.8 12.1 %gather_fusion.7 = bf16[4096,128]{1,0:T(8,128)(2,1)S(1)} fusion(bf16[8192,128]{1,0:T(8,128)(2,1)S(1)} %get-tuple-element.6, s32[4096]{0:T(1024)S(1)} %get-tuple-element.35), kind=kCustom, calls=%fused_computation.7.clone | custom fusion | bytes 2113536 | tf_op jit(solution)/shard_map/jit(_take)/gather | solution.py:19
  145.9 2.1 broadcast_select_fusion
  148.1 1.2 constant_dynamic-update-slice_fusion
  149.2 190.8 %all_to_all.10 = bf16[8,512,8,128]{3,1,2,0:T(8,128)(2,1)S(1)} all-to-all(bf16[8,512,8,128]{3,1,2,0:T(8,128)(2,1)} %constant_dynamic-update-slice_fusion), channel_id=1, replica_groups=mesh['batch'=8,'mp'=4] {'batch'}, dimensions={0} | all-to-all | bytes 16777216 | tf_op jit(solution)/shard_map/all_to_all | solution.py:29
  340.1 13.0 %slice_bitcast_fusion.3 = (bf16[1,8,512,8,32]{4,2,3,1,0:T(8,128)(2,1)}, bf16[1,8,512,8,32]{4,2,3,1,0:T(8,128)(2,1)}, bf16[1,8,512,8,32]{4,2,3,1,0:T(8,128)(2,1)}, bf16[1,8,512,8,32]{4,2,3,1,0:T(8,128)(2,1)}) fusion(bf16[8,512,8,128]{3,1,2,0:T(8,128)(2,1)S(1)} %all_to_all.10), kind=kLoop, calls=%fused_computation.16 | loop fusion | bytes 16777216 | tf_op jit(solution)/shard_map/stack | solution.py:27
  353.1 6.7 %copy.30 = bf16[1,8,512,8,32]{2,4,3,1,0:T(8,128)(2,1)S(1)} copy(bf16[1,8,512,8,32]{4,2,3,1,0:T(8,128)(2,1)} %get-tuple-element.14) | data formatting | bytes 4194304 | tf_op jit(solution)/shard_map/stack | solution.py:27
  359.8 8.1 %copy.31 = bf16[1,8,512,8,32]{2,4,3,1,0:T(8,128)(2,1)} copy(bf16[1,8,512,8,32]{4,2,3,1,0:T(8,128)(2,1)} %get-tuple-element.17) | data formatting | bytes 4194304 | tf_op jit(solution)/shard_map/stack | solution.py:27
  367.8 8.0 %copy.32 = bf16[1,8,512,8,32]{2,4,3,1,0:T(8,128)(2,1)} copy(bf16[1,8,512,8,32]{4,2,3,1,0:T(8,128)(2,1)} %get-tuple-element.16) | data formatting | bytes 4194304 | tf_op jit(solution)/shard_map/stack | solution.py:27
  375.9 8.0 %copy.33 = bf16[1,8,512,8,32]{2,4,3,1,0:T(8,128)(2,1)} copy(bf16[1,8,512,8,32]{4,2,3,1,0:T(8,128)(2,1)} %get-tuple-element.15) | data formatting | bytes 4194304 | tf_op jit(solution)/shard_map/stack | solution.py:27
  383.9 3.8 pad_maximum_fusion
  387.7 96.8 %all_to_all.11 = bf16[4,8,512,8,32]{2,4,3,1,0:T(8,128)(2,1)} all-to-all(bf16[4,8,512,8,32]{2,4,3,1,0:T(8,128)(2,1)S(1)} %pad_maximum_fusion), channel_id=1, replica_groups=mesh['batch'=8,'mp'=4] {'mp'}, dimensions={0} | all-to-all | bytes 16777216 | tf_op jit(solution)/shard_map/all_to_all | solution.py:26
  484.6 8.1 %copy.37 = bf16[4,8,8,4,8,512]{5,4,0,3,2,1:T(8,128)(2,1)} copy(bf16[4,8,8,4,8,512]{5,4,3,2,1,0:T(8,128)(2,1)} %bitcast.92) | data formatting | bytes 16777216 | tf_op jit(solution)/shard_map/reshape | solution.py:25
  492.7 10.1 %fusion.6 = bf16[2048,32,64]{0,2,1:T(8,128)(2,1)S(1)} fusion(bf16[2048,8,8,32]{0,3,2,1:T(8,128)(2,1)} %bitcast.91, s32[64]{0:T(128)S(1)} %copy-done.2), kind=kOutput, calls=%fused_computation.21 | convolution fusion | flops 541069312 | bytes 16777472 | tf_op jit(solution)/shard_map/rse,sf->ref/dot_general | solution.py:45
  502.8 3.4 copy-done
  506.2 7.4 %convolution_convert_fusion.1 = bf16[2048,512]{1,0:T(8,128)(2,1)} fusion(bf16[2048,2048]{0,1:T(8,128)(2,1)S(1)} %bitcast.89, bf16[2,2048,512]{2,1,0:T(8,128)(2,1)} %param.11), kind=kOutput, calls=%fused_computation.23 | convolution fusion | flops 4296015872 | bytes 12582912 | tf_op jit(solution)/shard_map/dot_general | solution.py:51
  513.5 0.0 all-reduce.3.cloned.1.call-update
  513.6 0.2 all-reduce.5.cloned.1.call-start
  513.8 11.7 %copy.36 = bf16[2048,2048]{1,0:T(8,128)(2,1)} copy(bf16[2048,2048]{0,1:T(8,128)(2,1)} %bitcast.90) | data formatting | bytes 16777216 | tf_op jit(solution)/shard_map/reshape | solution.py:46
  525.5 37.7 %all-reduce.3.cloned.1.call-done = bf16[2048,512]{1,0:T(8,128)(2,1)} async-done(((bf16[2048,512]{1,0:T(8,128)(2,1)}), bf16[2048,512]{1,0:T(8,128)(2,1)}) %all-reduce.3.cloned.1.call-update) | async-done | bytes 2097168 | tf_op jit(solution)/shard_map/psum | solution.py:53
  563.2 10.0 %fusion.2 = bf16[2048,2048]{1,0:T(8,128)(2,1)S(1)} fusion(bf16[2048,2048]{1,0:T(8,128)(2,1)} %copy.36, f32[2048]{0:T(1024)S(1)} %bitcast.119, bf16[2048,512]{1,0:T(8,128)(2,1)} %all-reduce.3.cloned.1.call-done, bf16[2,512,2048]{2,1,0:T(8,128)(2,1)} %param.12), kind=kOutput, calls=%fused_computation.12 | convolution fusion | flops 4315938816 | bytes 20979712 | tf_op jit(solution)/shard_map/dot_general | solution.py:55
  573.2 3.4 copy-done.4
  576.6 6.1 convolution_convert_fusion
  582.7 0.0 all-reduce.5.cloned.1.call-update
  582.7 51.6 %all-reduce.5.cloned.1.call-done = bf16[2048,512]{1,0:T(8,128)(2,1)} async-done(((bf16[2048,512]{1,0:T(8,128)(2,1)}), bf16[2048,512]{1,0:T(8,128)(2,1)}) %all-reduce.5.cloned.1.call-update) | async-done | bytes 2097168 | tf_op jit(solution)/shard_map/psum | solution.py:53
  634.4 15.9 %fusion.1 = bf16[2048,2048]{1,0:T(8,128)(2,1)} fusion(bf16[2048,2048]{1,0:T(8,128)(2,1)} %copy.36, bf16[2048,2048]{1,0:T(8,128)(2,1)} %copy-done.4, f32[2048]{0:T(1024)S(1)} %bitcast.118, bf16[2048,512]{1,0:T(8,128)(2,1)} %all-reduce.5.cloned.1.call-done, bf16[2,512,2048]{2,1,0:T(8,128)(2,1)} %param.12), kind=kOutput, calls=%fused_computation.11 | convolution fusion | flops 4320133120 | bytes 29368320 | tf_op jit(solution)/shard_map/dot_general | solution.py:55
  (22 shorter events, 0.2 us)
Async XLA Ops:
  6.5 556.7 %all-reduce.3.cloned.1.call-start = ((), (), s32[]{:S(2)}) async-start(), calls=%async_computation.2 | async-start | bytes 4194304 | tf_op jit(solution)/shard_map/psum | solution.py:53
  484.6 8.1 %copy-start.2 = (s32[64]{0:T(128)S(1)}, s32[64]{0:T(128)}, u32[]{:S(2)}) copy-start(s32[64]{0:T(128)} %param.9) | copy-start | bytes 772
  502.8 3.4 copy-start
  506.2 7.6 %copy-start.1 = (f32[2,2048]{1,0:T(2,128)S(1)}, f32[2,2048]{1,0:T(2,128)}, u32[]{:S(2)}) copy-start(f32[2,2048]{1,0:T(2,128)} %param.13) | copy-start | bytes 49156
  513.6 120.8 %all-reduce.5.cloned.1.call-start = ((), (), s32[]{:S(2)}) async-start(), calls=%async_computation.3 | async-start | bytes 4194304 | tf_op jit(solution)/shard_map/psum | solution.py:53
  563.2 13.4 %copy-start.3 = (bf16[2,2048,512]{2,1,0:T(8,128)(2,1)S(1)}, bf16[2,2048,512]{2,1,0:T(8,128)(2,1)}, u32[]{:S(2)}) copy-start(bf16[2,2048,512]{2,1,0:T(8,128)(2,1)} %param.11) | copy-start | bytes 12582916
  573.2 3.4 copy-start.4
Sparse Core Ops, SparseCore 0:
  513.7 49.4 all-reduce.2
  582.9 51.4 all-reduce.4
